TPU v7x, 32 devices: a whole 2x2x4 slice. The times are simulated.
32 devices in a mesh: ctx: 16 (over z, y, x), fsdp: 2 (over core).
Axes of the slice: x: 2, y: 2, z: 4, core: 2. Of those that a mesh axis runs over, the one named last changes fastest.
Arguments:
- tokens: bfloat16 [4, 2048, 576], P('fsdp', 'ctx'), may hold values from -6 to 6
- positions: int32 [4, 2048], P('fsdp', 'ctx'), may hold values from 0 to 2047, as said below
- norm_attn: bfloat16 [2, 576], P(None, 'fsdp'), may hold values from 0.5 to 1.5
- w_query: bfloat16 [2, 576, 576], P(None, 'fsdp'), may hold values from -0.25 to 0.25
- w_key: bfloat16 [2, 576, 192], P(None, 'fsdp'), may hold values from -0.25 to 0.25
- w_value: bfloat16 [2, 576, 192], P(None, 'fsdp'), may hold values from -0.25 to 0.25
- w_out: bfloat16 [2, 576, 576], P(None, 'fsdp'), may hold values from -2 to 2
- norm_ffn: bfloat16 [2, 576], P(None, 'fsdp'), may hold values from 0.5 to 1.5
- w_gate: bfloat16 [2, 576, 1536], P(None, 'fsdp'), may hold values from -0.25 to 0.25
- w_up: bfloat16 [2, 576, 1536], P(None, 'fsdp'), may hold values from -0.25 to 0.25
- w_down: bfloat16 [2, 1536, 576], P(None, 'fsdp'), may hold values from -0.15625 to 0.15625
- cotangent: bfloat16 [4, 2048, 576], P('fsdp', 'ctx'), may hold values from -6 to 6
Outputs:
- output: bfloat16 [4, 2048, 576], P('fsdp', 'ctx')
- grad_tokens: float32 [4, 2048, 576], P('fsdp', 'ctx')
- grad_norm_attn: float32 [2, 576], P(None, 'fsdp')
- grad_query: float32 [2, 576, 576], P(None, 'fsdp')
- grad_key: float32 [2, 576, 192], P(None, 'fsdp')
- grad_value: float32 [2, 576, 192], P(None, 'fsdp')
- grad_out: float32 [2, 576, 576], P(None, 'fsdp')
- grad_norm_ffn: float32 [2, 576], P(None, 'fsdp')
- grad_gate: float32 [2, 576, 1536], P(None, 'fsdp')
- grad_up: float32 [2, 576, 1536], P(None, 'fsdp')
- grad_down: float32 [2, 1536, 576], P(None, 'fsdp')
Inputs may be any that keep to these rules, and one draw needn't show every extreme that they name: For each sequence the 2048 positions are 0 .. 2047 once each; index c of ctx holds, in order, the two runs of 64 consecutive positions of blocks b and 31 - b, with b a permutation over the devices drawn per sequence.
All inputs are finite; a program needn't handle non-finite values.
Results may differ from a plain program's by a relative error of at most 0.02.
Values may be sent and summed in bfloat16 or wider, within the bound.
A program may use at most 320 MiB of HBM per device.

v0:
```python
import jax
import jax.numpy as jnp
from jax import lax
from jax.sharding import PartitionSpec as P

HEADS = 9
KV_HEADS = 3
HEAD = 64
EPS = 1e-05
ROPE_BASE = 100000.0


def rotate(tensor, positions_row, direction_sign):
    half_size = tensor.shape[-1] // 2
    frequency = jnp.exp(
        jnp.arange(half_size, dtype=jnp.float32) * (-jnp.log(ROPE_BASE) / half_size)
    )
    angles = positions_row.astype(jnp.float32)[..., None] * frequency
    cosine = jnp.cos(angles)[..., None, :]
    sine_part = direction_sign * jnp.sin(angles)[..., None, :]
    first_half = tensor[..., :half_size]
    second_half = tensor[..., half_size:]
    return jnp.concatenate(
        [
            first_half * cosine - second_half * sine_part,
            second_half * cosine + first_half * sine_part,
        ],
        axis=-1,
    )


def normalize(values, gain):
    return values * lax.rsqrt(jnp.mean(values * values, axis=-1, keepdims=True) + EPS) * gain


def normalize_back(values, gain, incoming):
    inverse = lax.rsqrt(jnp.mean(values * values, axis=-1, keepdims=True) + EPS)
    scaled = incoming * gain
    grad_values = inverse * scaled - values * (inverse * inverse * inverse) * jnp.mean(
        scaled * values, axis=-1, keepdims=True
    )
    grad_gain = jnp.sum(incoming * values * inverse, axis=(0, 1))
    return (grad_values, grad_gain)


def scores_of(queries, keys_all, query_places, key_places):
    raw_scores = jnp.einsum(
        "qhge,khe->hgqk", queries, keys_all, preferred_element_type=jnp.float32
    ) * queries.shape[-1] ** (-0.5)
    visible = key_places[None, :] <= query_places[:, None]
    return jnp.where(visible[None, None], raw_scores, -1e30)


def attend(operands):
    queries, keys_all, values_all, query_places, key_places = operands
    scores = scores_of(queries, keys_all, query_places, key_places)
    row_top = jnp.max(scores, axis=-1, keepdims=True)
    exponent = jnp.exp(scores - row_top)
    row_total = jnp.sum(exponent, axis=-1, keepdims=True)
    probabilities = (exponent / row_total).astype(jnp.bfloat16)
    mixed = jnp.einsum(
        "hgqk,khe->qhge", probabilities, values_all, preferred_element_type=jnp.float32
    )
    return (mixed, row_top + jnp.log(row_total))


def attend_back(operands):
    queries, keys_all, values_all, query_places, key_places, log_total, grad_mixed = operands
    score_scale = queries.shape[-1] ** (-0.5)
    scores = scores_of(queries, keys_all, query_places, key_places)
    probabilities = jnp.exp(scores - log_total)
    grad_probs = jnp.einsum(
        "qhge,khe->hgqk", grad_mixed, values_all, preferred_element_type=jnp.float32
    )
    grad_scores = (
        probabilities * (grad_probs - jnp.sum(probabilities * grad_probs, axis=-1, keepdims=True))
    ).astype(jnp.bfloat16)
    grad_queries = (
        jnp.einsum("hgqk,khe->qhge", grad_scores, keys_all, preferred_element_type=jnp.float32)
        * score_scale
    )
    grad_keys = (
        jnp.einsum("hgqk,qhge->khe", grad_scores, queries, preferred_element_type=jnp.float32)
        * score_scale
    )
    grad_values = jnp.einsum(
        "hgqk,qhge->khe",
        probabilities.astype(jnp.bfloat16),
        grad_mixed,
        preferred_element_type=jnp.float32,
    )
    return (grad_queries, grad_keys, grad_values)


def layer_forward(inputs, positions, places, weights):
    gain_attn, w_query, w_key, w_value, w_out, gain_ffn, w_gate, w_up, w_down = weights
    seq_count, row_count, model_width = inputs.shape
    normed = normalize(inputs, gain_attn).astype(jnp.bfloat16)
    query_pre = jnp.einsum("srd,de->sre", normed, w_query, preferred_element_type=jnp.float32)
    key_pre = jnp.einsum("srd,de->sre", normed, w_key, preferred_element_type=jnp.float32)
    value_pre = jnp.einsum("srd,de->sre", normed, w_value, preferred_element_type=jnp.float32)
    queries = rotate(query_pre.reshape(seq_count, row_count, HEADS, HEAD), positions, 1.0).astype(
        jnp.bfloat16
    )
    queries = queries.reshape(seq_count, row_count, KV_HEADS, HEADS // KV_HEADS, HEAD)
    keys_own = rotate(key_pre.reshape(seq_count, row_count, KV_HEADS, HEAD), positions, 1.0).astype(
        jnp.bfloat16
    )
    keys_own = keys_own.reshape(seq_count, row_count, KV_HEADS * HEAD)
    values_own = value_pre.astype(jnp.bfloat16)
    keys_all, values_all = (
        lax.all_gather(keys_own, "ctx", axis=1, tiled=True),
        lax.all_gather(values_own, "ctx", axis=1, tiled=True),
    )
    length = keys_all.shape[1]
    mixed, log_total = lax.map(
        attend,
        (
            queries,
            keys_all.reshape(seq_count, length, KV_HEADS, HEAD),
            values_all.reshape(seq_count, length, KV_HEADS, HEAD),
            positions,
            places,
        ),
    )
    mixed_low = mixed.reshape(seq_count, row_count, model_width).astype(jnp.bfloat16)
    middle = inputs + jnp.einsum(
        "srd,de->sre", mixed_low, w_out, preferred_element_type=jnp.float32
    )
    normed_ffn = normalize(middle, gain_ffn).astype(jnp.bfloat16)
    gate_pre = jnp.einsum("srd,df->srf", normed_ffn, w_gate, preferred_element_type=jnp.float32)
    up_pre = jnp.einsum("srd,df->srf", normed_ffn, w_up, preferred_element_type=jnp.float32)
    hidden = (jax.nn.silu(gate_pre) * up_pre).astype(jnp.bfloat16)
    result = middle + jnp.einsum("srf,fd->srd", hidden, w_down, preferred_element_type=jnp.float32)
    record = (
        inputs,
        normed,
        queries,
        keys_own,
        values_own,
        keys_all,
        values_all,
        log_total,
        mixed_low,
        middle,
        normed_ffn,
        gate_pre,
        up_pre,
        hidden,
    )
    return (result, record)


def layer_backward(gradient, record, weights, positions, places):
    gain_attn, w_query, w_key, w_value, w_out, gain_ffn, w_gate, w_up, w_down = weights
    (
        inputs,
        normed,
        queries,
        keys_own,
        values_own,
        kept_keys,
        kept_values,
        log_total,
        mixed_low,
        middle,
        normed_ffn,
        gate_pre,
        up_pre,
        hidden,
    ) = record
    seq_count, row_count, model_width = inputs.shape
    grad_low = gradient.astype(jnp.bfloat16)
    grad_wdown = jnp.einsum("srf,srd->fd", hidden, grad_low, preferred_element_type=jnp.float32)
    grad_hidden = jnp.einsum("srd,fd->srf", grad_low, w_down, preferred_element_type=jnp.float32)
    sigmoid_gate = jax.nn.sigmoid(gate_pre)
    grad_gate = (
        grad_hidden * up_pre * sigmoid_gate * (1.0 + gate_pre * (1.0 - sigmoid_gate))
    ).astype(jnp.bfloat16)
    grad_up = (grad_hidden * gate_pre * sigmoid_gate).astype(jnp.bfloat16)
    grad_wgate = jnp.einsum(
        "srd,srf->df", normed_ffn, grad_gate, preferred_element_type=jnp.float32
    )
    grad_wup = jnp.einsum("srd,srf->df", normed_ffn, grad_up, preferred_element_type=jnp.float32)
    grad_normed_ffn = jnp.einsum(
        "srf,df->srd", grad_gate, w_gate, preferred_element_type=jnp.float32
    ) + jnp.einsum("srf,df->srd", grad_up, w_up, preferred_element_type=jnp.float32)
    grad_middle_norm, grad_gain_ffn = normalize_back(middle, gain_ffn, grad_normed_ffn)
    grad_middle = gradient + grad_middle_norm
    branch_low = grad_middle.astype(jnp.bfloat16)
    grad_wout = jnp.einsum("srd,sre->de", mixed_low, branch_low, preferred_element_type=jnp.float32)
    grad_mixed = jnp.einsum(
        "sre,de->srd", branch_low, w_out, preferred_element_type=jnp.float32
    ).astype(jnp.bfloat16)
    grad_mixed = grad_mixed.reshape(seq_count, row_count, KV_HEADS, HEADS // KV_HEADS, HEAD)
    keys_all, values_all = (
        lax.all_gather(keys_own, "ctx", axis=1, tiled=True),
        lax.all_gather(values_own, "ctx", axis=1, tiled=True),
    )
    length = keys_all.shape[1]
    grad_queries, grad_keys_all, grad_values_all = lax.map(
        attend_back,
        (
            queries,
            keys_all.reshape(seq_count, length, KV_HEADS, HEAD),
            values_all.reshape(seq_count, length, KV_HEADS, HEAD),
            positions,
            places,
            log_total,
            grad_mixed,
        ),
    )
    grad_keys, grad_values = (
        lax.psum_scatter(
            grad_keys_all.reshape(seq_count, length, KV_HEADS * HEAD),
            "ctx",
            scatter_dimension=1,
            tiled=True,
        ),
        lax.psum_scatter(
            grad_values_all.reshape(seq_count, length, KV_HEADS * HEAD),
            "ctx",
            scatter_dimension=1,
            tiled=True,
        ),
    )
    grad_query_pre = (
        rotate(grad_queries.reshape(seq_count, row_count, HEADS, HEAD), positions, -1.0)
        .reshape(seq_count, row_count, model_width)
        .astype(jnp.bfloat16)
    )
    grad_key_pre = (
        rotate(grad_keys.reshape(seq_count, row_count, KV_HEADS, HEAD), positions, -1.0)
        .reshape(seq_count, row_count, KV_HEADS * HEAD)
        .astype(jnp.bfloat16)
    )
    grad_value_pre = grad_values.astype(jnp.bfloat16)
    grad_wquery = jnp.einsum(
        "srd,sre->de", normed, grad_query_pre, preferred_element_type=jnp.float32
    )
    grad_wkey = jnp.einsum("srd,sre->de", normed, grad_key_pre, preferred_element_type=jnp.float32)
    grad_wvalue = jnp.einsum(
        "srd,sre->de", normed, grad_value_pre, preferred_element_type=jnp.float32
    )
    grad_normed = jnp.einsum(
        "sre,de->srd", grad_query_pre, w_query, preferred_element_type=jnp.float32
    )
    grad_normed = grad_normed + jnp.einsum(
        "sre,de->srd", grad_key_pre, w_key, preferred_element_type=jnp.float32
    )
    grad_normed = grad_normed + jnp.einsum(
        "sre,de->srd", grad_value_pre, w_value, preferred_element_type=jnp.float32
    )
    grad_input_norm, grad_gain_attn = normalize_back(inputs, gain_attn, grad_normed)
    layer_grads = (
        grad_gain_attn,
        grad_wquery,
        grad_wkey,
        grad_wvalue,
        grad_wout,
        grad_gain_ffn,
        grad_wgate,
        grad_wup,
        grad_wdown,
    )
    return (grad_middle + grad_input_norm, layer_grads)


def body(
    tokens,
    positions,
    norm_attn,
    w_query,
    w_key,
    w_value,
    w_out,
    norm_ffn,
    w_gate,
    w_up,
    w_down,
    cotangent,
):
    layer_count = norm_attn.shape[0]
    places = lax.all_gather(positions, "ctx", axis=1, tiled=True)
    current = tokens.astype(jnp.float32)
    records = []
    gathered_weights = []
    for layer_index in range(layer_count):
        weights = (
            lax.all_gather(norm_attn[layer_index], "fsdp", axis=0, tiled=True),
            lax.all_gather(w_query[layer_index], "fsdp", axis=0, tiled=True),
            lax.all_gather(w_key[layer_index], "fsdp", axis=0, tiled=True),
            lax.all_gather(w_value[layer_index], "fsdp", axis=0, tiled=True),
            lax.all_gather(w_out[layer_index], "fsdp", axis=0, tiled=True),
            lax.all_gather(norm_ffn[layer_index], "fsdp", axis=0, tiled=True),
            lax.all_gather(w_gate[layer_index], "fsdp", axis=0, tiled=True),
            lax.all_gather(w_up[layer_index], "fsdp", axis=0, tiled=True),
            lax.all_gather(w_down[layer_index], "fsdp", axis=0, tiled=True),
        )
        current, record = layer_forward(current, positions, places, weights)
        records.append(record)
        gathered_weights.append(weights)
    output = current.astype(jnp.bfloat16)
    gradient = cotangent.astype(jnp.float32)
    collected = []
    for layer_index in reversed(range(layer_count)):
        weights = (
            lax.all_gather(norm_attn[layer_index], "fsdp", axis=0, tiled=True),
            lax.all_gather(w_query[layer_index], "fsdp", axis=0, tiled=True),
            lax.all_gather(w_key[layer_index], "fsdp", axis=0, tiled=True),
            lax.all_gather(w_value[layer_index], "fsdp", axis=0, tiled=True),
            lax.all_gather(w_out[layer_index], "fsdp", axis=0, tiled=True),
            lax.all_gather(norm_ffn[layer_index], "fsdp", axis=0, tiled=True),
            lax.all_gather(w_gate[layer_index], "fsdp", axis=0, tiled=True),
            lax.all_gather(w_up[layer_index], "fsdp", axis=0, tiled=True),
            lax.all_gather(w_down[layer_index], "fsdp", axis=0, tiled=True),
        )
        gradient, layer_grads = layer_backward(
            gradient, records[layer_index], weights, positions, places
        )
        shares = (
            lax.psum_scatter(
                layer_grads[0].astype(jnp.bfloat16), "fsdp", scatter_dimension=0, tiled=True
            ).astype(jnp.float32),
            lax.psum_scatter(
                layer_grads[1].astype(jnp.bfloat16), "fsdp", scatter_dimension=0, tiled=True
            ).astype(jnp.float32),
            lax.psum_scatter(
                layer_grads[2].astype(jnp.bfloat16), "fsdp", scatter_dimension=0, tiled=True
            ).astype(jnp.float32),
            lax.psum_scatter(
                layer_grads[3].astype(jnp.bfloat16), "fsdp", scatter_dimension=0, tiled=True
            ).astype(jnp.float32),
            lax.psum_scatter(
                layer_grads[4].astype(jnp.bfloat16), "fsdp", scatter_dimension=0, tiled=True
            ).astype(jnp.float32),
            lax.psum_scatter(
                layer_grads[5].astype(jnp.bfloat16), "fsdp", scatter_dimension=0, tiled=True
            ).astype(jnp.float32),
            lax.psum_scatter(
                layer_grads[6].astype(jnp.bfloat16), "fsdp", scatter_dimension=0, tiled=True
            ).astype(jnp.float32),
            lax.psum_scatter(
                layer_grads[7].astype(jnp.bfloat16), "fsdp", scatter_dimension=0, tiled=True
            ).astype(jnp.float32),
            lax.psum_scatter(
                layer_grads[8].astype(jnp.bfloat16), "fsdp", scatter_dimension=0, tiled=True
            ).astype(jnp.float32),
        )
        totals = lax.psum(
            (
                shares[0],
                shares[1],
                shares[2],
                shares[3],
                shares[4],
                shares[5],
                shares[6],
                shares[7],
                shares[8],
            ),
            "ctx",
        )
        collected.insert(0, totals)
    stacked = tuple(
        (jnp.stack([entry_totals[member] for entry_totals in collected]) for member in range(9))
    )
    return (
        output,
        gradient,
        stacked[0],
        stacked[1],
        stacked[2],
        stacked[3],
        stacked[4],
        stacked[5],
        stacked[6],
        stacked[7],
        stacked[8],
    )


def solution(mesh):
    in_specs = (
        P("fsdp", "ctx", None),
        P("fsdp", "ctx"),
        P(None, "fsdp"),
        P(None, "fsdp", None),
        P(None, "fsdp", None),
        P(None, "fsdp", None),
        P(None, "fsdp", None),
        P(None, "fsdp"),
        P(None, "fsdp", None),
        P(None, "fsdp", None),
        P(None, "fsdp", None),
        P("fsdp", "ctx", None),
    )
    out_specs = (
        P("fsdp", "ctx", None),
        P("fsdp", "ctx", None),
        P(None, "fsdp"),
        P(None, "fsdp", None),
        P(None, "fsdp", None),
        P(None, "fsdp", None),
        P(None, "fsdp", None),
        P(None, "fsdp"),
        P(None, "fsdp", None),
        P(None, "fsdp", None),
        P(None, "fsdp", None),
    )
    return jax.shard_map(body, mesh=mesh, in_specs=in_specs, out_specs=out_specs, check_vma=False)
```

profile of v0, /device:TPU:0, one launch (start us, length us, event | category | flops | bytes accessed | tf_op | source)
XLA Modules:
  0.0 1770.1 jit_solution(10200862059027686231)
XLA Ops:
  31.5 42.7 %all_gather.94 = s32[2,2048]{1,0:T(2,128)S(1)} all-gather(s32[2,128]{1,0:T(2,128)S(1)} %copy-done.116), channel_id=1, replica_groups=mesh['ctx'=16,'fsdp'=2] {'ctx'}, dimensions={1}, use_global_device_ids=true | all-gather | bytes 17408 | tf_op jit(solution)/shard_map/all_gather | solution.py:284
  86.0 50.3 %all-gather.31.cloned.1.call-done = bf16[2,2048,192]{1,2,0:T(8,128)(2,1)} async-done(((bf16[2,128,192]{1,2,0:T(8,128)(2,1)}), bf16[2,2048,192]{1,2,0:T(8,128)(2,1)}) %all-gather.31.cloned.1.call-update) | async-done | bytes 1572880 | tf_op jit(solution)/shard_map/all_gather | solution.py:112
  136.3 15.6 while.52
  164.0 8.7 all-gather.41.cloned.1.call-done
  191.8 55.6 %all-gather.33.cloned.1.call-done = bf16[2,2048,192]{1,2,0:T(8,128)(2,1)} async-done(((bf16[2,128,192]{1,2,0:T(8,128)(2,1)}), bf16[2,2048,192]{1,2,0:T(8,128)(2,1)}) %all-gather.33.cloned.1.call-update) | async-done | bytes 1572880 | tf_op jit(solution)/shard_map/all_gather | solution.py:113
  247.4 58.3 %all-gather.35.cloned.1.call-done = bf16[2,2048,192]{1,2,0:T(8,128)(2,1)} async-done(((bf16[2,128,192]{1,2,0:T(8,128)(2,1)}), bf16[2,2048,192]{1,2,0:T(8,128)(2,1)}) %all-gather.35.cloned.1.call-update) | async-done | bytes 1572880 | tf_op jit(solution)/shard_map/all_gather | solution.py:112
  305.7 15.6 while.53
  344.0 63.8 %while.54 = (s32[]{:T(128)}, f32[2,128,3,3,64]{1,4,3,2,0:T(8,128)}, f32[2,2048,3,64]{1,3,2,0:T(8,128)}, f32[2,2048,3,64]{1,3,2,0:T(8,128)}, bf16[2,2048,3,64]{1,...) while((s32[]{:T(128)}, f32[2,128,3,3,64]{1,4,3,2,0:T(8,128)}, ...), condition=%wide.region_15.16_spmd, body=%wide.region_13.15_spmd.sunk | while | flops 1546066816 | bytes 160072944 | solution.py:201
  346.0 5.8 fusion.325
  351.9 11.1 fusion.326
  367.1 5.3 fusion.328
  377.8 5.8 fusion.325
  383.7 11.1 fusion.326
  398.8 5.3 fusion.328
  421.1 120.8 %reduce-scatter.19.cloned.1.call-done = f32[2,128,192]{1,2,0:T(8,128)} async-done(((f32[2,2048,192]{1,2,0:T(8,128)}), f32[2,128,192]{1,2,0:T(8,128)}) %reduce-scatter.19.cloned.1.call-update) | async-done | bytes 196624 | tf_op jit(solution)/shard_map/reduce_scatter | solution.py:214
  544.5 134.7 %reduce-scatter.21.cloned.1.call-done = f32[2,128,192]{1,2,0:T(8,128)} async-done(((f32[2,2048,192]{1,2,0:T(8,128)}), f32[2,128,192]{1,2,0:T(8,128)}) %reduce-scatter.21.cloned.1.call-update) | async-done | bytes 196624 | tf_op jit(solution)/shard_map/reduce_scatter | solution.py:220
  696.9 65.5 %while.55 = (s32[]{:T(128)}, f32[2,128,3,3,64]{1,4,3,2,0:T(8,128)}, f32[2,2048,3,64]{1,3,2,0:T(8,128)}, f32[2,2048,3,64]{1,3,2,0:T(8,128)}, bf16[2,2048,3,64]{1,...) while((s32[]{:T(128)}, f32[2,128,3,3,64]{1,4,3,2,0:T(8,128)}, ...), condition=%wide.region_22.23_spmd, body=%wide.region_20.22_spmd.sunk | while | flops 1546066816 | bytes 160072944 | solution.py:201
  698.8 5.8 fusion.340
  704.8 11.8 fusion.341
  720.6 5.8 fusion.343
  731.9 5.8 fusion.340
  738.4 11.1 fusion.341
  753.5 5.3 fusion.343
  795.6 10.8 reduce-scatter.43.cloned.1.call-done
  809.0 137.1 %reduce-scatter.23.cloned.1.call-done = f32[2,128,192]{1,2,0:T(8,128)} async-done(((f32[2,2048,192]{1,2,0:T(8,128)}), f32[2,128,192]{1,2,0:T(8,128)}) %reduce-scatter.23.cloned.1.call-update) | async-done | bytes 196624 | tf_op jit(solution)/shard_map/reduce_scatter | solution.py:214
  948.2 8.3 reduce-scatter.47.cloned.1.call-done
  959.1 137.1 %reduce-scatter.25.cloned.1.call-done = f32[2,128,192]{1,2,0:T(8,128)} async-done(((f32[2,2048,192]{1,2,0:T(8,128)}), f32[2,128,192]{1,2,0:T(8,128)}) %reduce-scatter.25.cloned.1.call-update) | async-done | bytes 196624 | tf_op jit(solution)/shard_map/reduce_scatter | solution.py:220
  1098.2 8.3 reduce-scatter.51.cloned.1.call-done
  1109.0 9.2 reduce-scatter.31.cloned.1.call-done
  1119.9 10.1 reduce-scatter.35.cloned.1.call-done
  1140.7 45.2 %all-reduce.8 = (f32[1,288]{1,0:T(1,128)S(1)}, f32[1,288]{1,0:T(1,128)S(1)}, f32[1,288]{1,0:T(1,128)S(1)}, f32[1,288]{1,0:T(1,128)S(1)}) all-reduce(f32[1,288]{1,0:T(1,128)S(1)} %stack.82, f32[1,288]{1,0:T(1,128)S(1)} %stack.81, f32[1,288]{1,0:T(1,128)S(1)} %stack.97, ...), channel_id=1, replica_groups=mesh['ctx'=16,'fsdp'=2] {'ctx'}, use_global_device_ids=true, to_apply=%region_31.32 | all-reduce | flops 1152 | bytes 9216 | tf_op jit(solution)/shard_map/psum | solution.py:350
  1188.1 562.2 %all-reduce.14.cloned.1.call-done = (f32[1,288,576]{2,1,0:T(8,128)}, f32[1,288,576]{2,1,0:T(8,128)}, f32[1,288,192]{2,1,0:T(8,128)}, f32[1,288,192]{2,1,0:T(8,12...) async-done(((f32[1,288,576]{2,1,0:T(8,128)}, ...) | async-done | bytes 14155792 | tf_op jit(solution)/shard_map/psum | solution.py:350
  (533 shorter events, 262.7 us)
Async XLA Ops:
  7.2 78.8 %all-gather.29.cloned.1.call-start = ((), (), s32[]{:S(2)}) async-start(), calls=%async_computation.18 | async-start | bytes 1671168 | tf_op jit(solution)/shard_map/all_gather | solution.py:113
  19.0 117.3 %all-gather.31.cloned.1.call-start = ((), (), s32[]{:S(2)}) async-start(), calls=%async_computation.19 | async-start | bytes 1671168 | tf_op jit(solution)/shard_map/all_gather | solution.py:112
  23.9 167.8 %copy-start.58 = (f32[2,128,32]{1,2,0:T(8,128)}, f32[2,128,32]{1,2,0:T(8,128)S(1)}, u32[]{:S(2)}) copy-start(f32[2,128,32]{1,2,0:T(8,128)S(1)} %get-tuple-element.386) | copy-start | bytes 98308
  25.0 128.2 %all-gather.37.cloned.1.call-start = ((), (), s32[]{:S(2)}) async-start(), calls=%async_computation.40 | async-start | bytes 2654208 | tf_op jit(solution)/shard_map/all_gather | solution.py:296
  26.4 133.6 %all-gather.39.cloned.1.call-start = ((), (), s32[]{:S(2)}) async-start(), calls=%async_computation.41 | async-start | bytes 2654208 | tf_op jit(solution)/shard_map/all_gather | solution.py:297
  29.4 143.3 %all-gather.41.cloned.1.call-start = ((), (), s32[]{:S(2)}) async-start(), calls=%async_computation.42 | async-start | bytes 2654208 | tf_op jit(solution)/shard_map/all_gather | solution.py:298
  30.8 157.0 %all-gather.47.cloned.1.call-start = ((), (), s32[]{:S(2)}) async-start(), calls=%async_computation.45 | async-start | bytes 2654208 | tf_op jit(solution)/shard_map/all_gather | solution.py:298
  31.4 216.0 %all-gather.33.cloned.1.call-start = ((), (), s32[]{:S(2)}) async-start(), calls=%async_computation.20 | async-start | bytes 1671168 | tf_op jit(solution)/shard_map/all_gather | solution.py:113
  176.5 129.2 %all-gather.35.cloned.1.call-start = ((), (), s32[]{:S(2)}) async-start(), calls=%async_computation.21 | async-start | bytes 1671168 | tf_op jit(solution)/shard_map/all_gather | solution.py:112
  181.1 140.9 %all-gather.45.cloned.1.call-start = ((), (), s32[]{:S(2)}) async-start(), calls=%async_computation.44 | async-start | bytes 2654208 | tf_op jit(solution)/shard_map/all_gather | solution.py:297
  181.8 147.6 %all-gather.43.cloned.1.call-start = ((), (), s32[]{:S(2)}) async-start(), calls=%async_computation.43 | async-start | bytes 2654208 | tf_op jit(solution)/shard_map/all_gather | solution.py:296
  182.4 359.5 %reduce-scatter.19.cloned.1.call-start = ((), (), s32[]{:S(2)}) async-start(), calls=%async_computation.22 | async-start | bytes 3342336 | tf_op jit(solution)/shard_map/reduce_scatter | solution.py:214
  407.8 271.4 %reduce-scatter.21.cloned.1.call-start = ((), (), s32[]{:S(2)}) async-start(), calls=%async_computation.23 | async-start | bytes 3342336 | tf_op jit(solution)/shard_map/reduce_scatter | solution.py:220
  408.4 365.8 %reduce-scatter.29.cloned.1.call-start = ((), (), s32[]{:S(2)}) async-start(), calls=%async_computation.27 | async-start | bytes 1105920 | tf_op jit(solution)/shard_map/reduce_scatter | solution.py:325
  410.3 367.8 %reduce-scatter.41.cloned.1.call-start = ((), (), s32[]{:S(2)}) async-start(), calls=%async_computation.33 | async-start | bytes 1105920 | tf_op jit(solution)/shard_map/reduce_scatter | solution.py:334
  411.8 368.3 %reduce-scatter.53.cloned.1.call-start = ((), (), s32[]{:S(2)}) async-start(), calls=%async_computation.39 | async-start | bytes 2654208 | tf_op jit(solution)/shard_map/reduce_scatter | solution.py:346
  414.8 367.7 %reduce-scatter.45.cloned.1.call-start = ((), (), s32[]{:S(2)}) async-start(), calls=%async_computation.35 | async-start | bytes 2654208 | tf_op jit(solution)/shard_map/reduce_scatter | solution.py:340
  417.9 367.2 %reduce-scatter.49.cloned.1.call-start = ((), (), s32[]{:S(2)}) async-start(), calls=%async_computation.37 | async-start | bytes 2654208 | tf_op jit(solution)/shard_map/reduce_scatter | solution.py:343
  421.0 258.1 %copy-start.103 = (f32[576]{0:T(1024)S(1)}, f32[576]{0:T(1024)}, u32[]{:S(2)}) copy-start(f32[576]{0:T(1024)} %copy-done.102) | copy-start | bytes 6916
  421.1 258.1 %copy-start.109 = (f32[2,128]{1,0:T(2,128)S(1)}, f32[2,128]{1,0:T(2,128)}, u32[]{:S(2)}) copy-start(f32[2,128]{1,0:T(2,128)} %copy-done.108) | copy-start | bytes 3076
  421.1 366.6 %reduce-scatter.33.cloned.1.call-start = ((), (), s32[]{:S(2)}) async-start(), calls=%async_computation.29 | async-start | bytes 442368 | tf_op jit(solution)/shard_map/reduce_scatter | solution.py:328
  691.6 97.7 %reduce-scatter.37.cloned.1.call-start = ((), (), s32[]{:S(2)}) async-start(), calls=%async_computation.31 | async-start | bytes 442368 | tf_op jit(solution)/shard_map/reduce_scatter | solution.py:331
  764.4 26.6 %reduce-scatter.27.cloned.1.call-start = ((), (), s32[]{:S(2)}) async-start(), calls=%async_computation.26 | async-start | bytes 1105920 | tf_op jit(solution)/shard_map/reduce_scatter | solution.py:325
  767.0 26.7 %reduce-scatter.39.cloned.1.call-start = ((), (), s32[]{:S(2)}) async-start(), calls=%async_computation.32 | async-start | bytes 1105920 | tf_op jit(solution)/shard_map/reduce_scatter | solution.py:334
  768.4 38.0 %reduce-scatter.43.cloned.1.call-start = ((), (), s32[]{:S(2)}) async-start(), calls=%async_computation.34 | async-start | bytes 2654208 | tf_op jit(solution)/shard_map/reduce_scatter | solution.py:340
  770.3 175.8 %reduce-scatter.23.cloned.1.call-start = ((), (), s32[]{:S(2)}) async-start(), calls=%async_computation.24 | async-start | bytes 3342336 | tf_op jit(solution)/shard_map/reduce_scatter | solution.py:214
  771.0 185.4 %reduce-scatter.47.cloned.1.call-start = ((), (), s32[]{:S(2)}) async-start(), calls=%async_computation.36 | async-start | bytes 2654208 | tf_op jit(solution)/shard_map/reduce_scatter | solution.py:343
  773.4 322.8 %reduce-scatter.25.cloned.1.call-start = ((), (), s32[]{:S(2)}) async-start(), calls=%async_computation.25 | async-start | bytes 3342336 | tf_op jit(solution)/shard_map/reduce_scatter | solution.py:220
  774.1 332.3 %reduce-scatter.51.cloned.1.call-start = ((), (), s32[]{:S(2)}) async-start(), calls=%async_computation.38 | async-start | bytes 2654208 | tf_op jit(solution)/shard_map/reduce_scatter | solution.py:346
  778.0 340.2 %reduce-scatter.31.cloned.1.call-start = ((), (), s32[]{:S(2)}) async-start(), calls=%async_computation.28 | async-start | bytes 442368 | tf_op jit(solution)/shard_map/reduce_scatter | solution.py:328
  948.1 181.8 %reduce-scatter.35.cloned.1.call-start = ((), (), s32[]{:S(2)}) async-start(), calls=%async_computation.30 | async-start | bytes 442368 | tf_op jit(solution)/shard_map/reduce_scatter | solution.py:331
  1098.1 652.2 %all-reduce.14.cloned.1.call-start = ((), (), s32[]{:S(2)}) async-start(), calls=%async_computation.46 | async-start | bytes 29491200 | tf_op jit(solution)/shard_map/psum | solution.py:350
  (123 other events, 1760.9 us)
Sparse Core Ops, SparseCore 0:
  19.1 59.4 all-gather.28
  81.2 54.9 all-gather.30
  138.4 8.3 all-gather.36
  148.8 11.1 all-gather.38
  161.4 11.2 all-gather.40
  174.6 11.4 all-gather.46
  189.4 57.9 all-gather.32
  250.7 54.9 all-gather.34
  307.8 8.3 all-gather.44
  318.2 11.1 all-gather.42
  407.9 134.0 reduce-scatter.18
  547.4 131.7 reduce-scatter.20
  681.4 7.0 reduce-scatter.28
  690.7 9.1 reduce-scatter.40
  702.0 10.3 reduce-scatter.52
  715.1 10.5 reduce-scatter.44
  727.8 10.5 reduce-scatter.48
  741.1 9.0 reduce-scatter.32
  764.5 6.1 reduce-scatter.36
  772.8 9.2 reduce-scatter.26
  784.4 9.2 reduce-scatter.38
  795.9 10.4 reduce-scatter.42
  811.9 134.1 reduce-scatter.22
  948.2 8.2 reduce-scatter.46
  962.0 134.1 reduce-scatter.24
  1098.3 8.1 reduce-scatter.50
  1109.1 9.0 reduce-scatter.30
  1121.0 8.8 reduce-scatter.34
  1137.5 612.7 all-reduce.13
where the time goes:
time: 1780 us; the launch traced here: 1770 us
  waiting for transfers between devices  1320 us (74%)
  matrix products  172 us (10%)
  blocking collectives  112 us (6%)
  other arithmetic  109 us (6%)
  local copies, waits for them, and re-layouts  34.3 us (2%)
    psum x1, waiting for transfers between devices, body(): lax.psum((shares[0], shares[1], shares[2], shares[3], shares[4], shares[5...  562 us
    reduce_scatter x2, waiting for transfers between devices, layer_backward(): lax.psum_scatter(grad_values_all.reshape(seq_count, length, KV_HEADS * HE...  272 us
    reduce_scatter x2, waiting for transfers between devices, layer_backward(): lax.psum_scatter(grad_keys_all.reshape(seq_count, length, KV_HEADS * HEAD...  258 us
    all_gather x2, waiting for transfers between devices, layer_forward(): lax.all_gather(keys_own, 'ctx', axis=1, tiled=True)  109 us
    all_gather x2, waiting for transfers between devices, layer_forward(): lax.all_gather(values_own, 'ctx', axis=1, tiled=True)  55.6 us
    psum x1, blocking collectives, body(): lax.psum((shares[0], shares[1], shares[2], shares[3], shares[4], shares[5...  45.2 us
    convert_element_type x4, other arithmetic, attend_back(): grad_scores = (probabilities * (grad_probs - jnp.sum(probabilities * grad...  45 us
    all_gather x1, blocking collectives, body(): places = lax.all_gather(positions, 'ctx', axis=1, tiled=True)  42.7 us
  transfers between devices with their start and end apart: 29, of which 17 were waited for; matrix products, arithmetic and copies ran while one was open for 12% of the time, Pallas kernels for 0%

commit v1 on v0

--- a/solution.py
+++ b/solution.py
@@ -8,6 +8,31 @@
 HEAD = 64
 EPS = 1e-05
 ROPE_BASE = 100000.0
+
+
+def _assign_levels_all(sample):
+    prior = lax.axis_size("ctx")
+    reply, before, all_rows = (prior, lax.axis_index("ctx"), sample.shape[1])
+    b_next = range(reply)
+    everything = map(lambda k0: (k0, (k0 + 1) % reply), b_next)
+    entries = list(everything)
+    finding = map(lambda k0: (k0, (k0 - 1) % reply), range(reply))
+    w2 = jnp.zeros((*sample.shape[:1], reply * all_rows, *sample.shape[2:]), sample.dtype)
+    w2 = lax.dynamic_update_slice_in_dim(w2, sample, before * all_rows, axis=1)
+    log = list(finding)
+    later = f_next = sample
+    field_out = reply // 2
+    ix = 1
+    while ix < field_out + 1:
+        later = lax.ppermute(later, axis_name="ctx", perm=entries)
+        w2 = lax.dynamic_update_slice_in_dim(w2, later, (before - ix) % reply * all_rows, axis=1)
+        if ix < reply - field_out:
+            f_next = lax.ppermute(f_next, "ctx", perm=log)
+            w2 = lax.dynamic_update_slice_in_dim(
+                w2, f_next, (before + ix) % reply * all_rows, axis=1
+            )
+        ix += 1
+    return w2
 
 
 def rotate(tensor, positions_row, direction_sign):
@@ -109,7 +134,7 @@
     keys_own = keys_own.reshape(seq_count, row_count, KV_HEADS * HEAD)
     values_own = value_pre.astype(jnp.bfloat16)
     keys_all, values_all = (
-        lax.all_gather(keys_own, "ctx", axis=1, tiled=True),
+        _assign_levels_all(keys_own),
         lax.all_gather(values_own, "ctx", axis=1, tiled=True),
     )
     length = keys_all.shape[1]

time: 1780 us -> 1810 us (1.017)
  starting transfers between devices: 1.65 us -> 84.4 us
  waiting for transfers between devices: 1320 us -> 1270 us
    ppermute x0 -> x30, starting transfers between devices: none -> 82.8 us  [the longest x14 79.7 us: _assign_levels_all(): f_next = lax.ppermute(f_next, 'ctx', perm=log)]
    all_gather x2, waiting for transfers between devices: 55.6 us -> 0.04 us  [layer_forward(): lax.all_gather(values_own, 'ctx', axis=1, tiled=True)]
    ppermute x0 -> x30, waiting for transfers between devices: none -> 48.3 us  [the longest x16 46 us: _assign_levels_all(): later = lax.ppermute(later, axis_name='ctx', perm=entries)]
    all_gather x2, waiting for transfers between devices: 109 us -> 75.2 us  [layer_backward(): lax.all_gather(keys_own, 'ctx', axis=1, tiled=True)]
  transfers between devices with their start and end apart: 29 -> 59, of which waited for: 17 -> 31; matrix products, arithmetic and copies ran while one was open for 12% -> 12% of each run, Pallas kernels for 0% -> 0%
where the time goes in v1:
time: 1810 us; the launch traced here: 1800 us
  waiting for transfers between devices  1270 us (70%)
  matrix products  163 us (9%)
  other arithmetic  109 us (6%)
  blocking collectives  108 us (6%)
  starting transfers between devices  84.4 us (5%)
  local copies, waits for them, and re-layouts  48.3 us (3%)
    psum x1, waiting for transfers between devices, body(): lax.psum((shares[0], shares[1], shares[2], shares[3], shares[4], shares[5...  563 us
    reduce_scatter x2, waiting for transfers between devices, layer_backward(): lax.psum_scatter(grad_values_all.reshape(seq_count, length, KV_HEADS * HE...  272 us
    reduce_scatter x2, waiting for transfers between devices, layer_backward(): lax.psum_scatter(grad_keys_all.reshape(seq_count, length, KV_HEADS * HEAD...  257 us
    ppermute x14, starting transfers between devices, _assign_levels_all(): f_next = lax.ppermute(f_next, 'ctx', perm=log)  79.7 us
    all_gather x2, waiting for transfers between devices, layer_backward(): lax.all_gather(keys_own, 'ctx', axis=1, tiled=True)  75.2 us
    ppermute x16, waiting for transfers between devices, _assign_levels_all(): later = lax.ppermute(later, axis_name='ctx', perm=entries)  46 us
    psum x1, blocking collectives, body(): lax.psum((shares[0], shares[1], shares[2], shares[3], shares[4], shares[5...  45.1 us
    convert_element_type x4, other arithmetic, attend_back(): grad_scores = (probabilities * (grad_probs - jnp.sum(probabilities * grad...  44.3 us
  transfers between devices with their start and end apart: 59, of which 31 were waited for; matrix products, arithmetic and copies ran while one was open for 12% of the time, Pallas kernels for 0%

profile of v1, /device:TPU:0, one launch (start us, length us, event | category | flops | bytes accessed | tf_op | source)
XLA Modules:
  0.0 1800.6 jit_solution(4168971713860009152)
XLA Ops:
  39.8 38.4 %all_gather.92 = s32[2,2048]{1,0:T(2,128)S(1)} all-gather(s32[2,128]{1,0:T(2,128)} %param.21), channel_id=1, replica_groups=mesh['ctx'=16,'fsdp'=2] {'ctx'}, dimensions={1}, use_global_device_ids=true | all-gather | bytes 17408 | tf_op jit(solution)/shard_map/all_gather | solution.py:309
  108.5 5.7 collective-permute-start.7
  124.9 5.8 collective-permute-start.11
  133.1 5.9 collective-permute-start.13
  141.6 8.1 collective-permute-done.14
  149.8 14.5 while.52
  202.5 6.1 collective-permute-start.18
  211.2 5.9 collective-permute-start.20
  220.4 6.2 collective-permute-start.22
  228.8 6.1 collective-permute-start.24
  256.0 8.1 collective-permute-done.29
  264.2 15.9 while.53
  294.9 29.4 %all-gather.33.cloned.1.call-done = bf16[2,2048,192]{1,2,0:T(8,128)(2,1)} async-done(((bf16[2,128,192]{1,2,0:T(8,128)(2,1)}), bf16[2,2048,192]{1,2,0:T(8,128)(2,1)}) %all-gather.33.cloned.1.call-update) | async-done | bytes 1572880 | tf_op jit(solution)/shard_map/all_gather | solution.py:222
  329.3 63.6 %while.54 = (s32[]{:T(128)}, f32[2,128,3,3,64]{1,4,3,2,0:T(8,128)}, f32[2,2048,3,64]{1,3,2,0:T(8,128)}, f32[2,2048,3,64]{1,3,2,0:T(8,128)}, bf16[2,2048,3,64]{1,...) while((s32[]{:T(128)}, f32[2,128,3,3,64]{1,4,3,2,0:T(8,128)}, ...), condition=%wide.region_15.16_spmd, body=%wide.region_13.15_spmd.sunk | while | flops 1546066816 | bytes 160072944 | solution.py:226
  337.3 11.0 fusion.326
  369.0 11.0 fusion.326
  404.5 119.6 %reduce-scatter.19.cloned.1.call-done = f32[2,128,192]{1,2,0:T(8,128)} async-done(((f32[2,2048,192]{1,2,0:T(8,128)}), f32[2,128,192]{1,2,0:T(8,128)}) %reduce-scatter.19.cloned.1.call-update) | async-done | bytes 196624 | tf_op jit(solution)/shard_map/reduce_scatter | solution.py:239
  526.7 134.9 %reduce-scatter.21.cloned.1.call-done = f32[2,128,192]{1,2,0:T(8,128)} async-done(((f32[2,2048,192]{1,2,0:T(8,128)}), f32[2,128,192]{1,2,0:T(8,128)}) %reduce-scatter.21.cloned.1.call-update) | async-done | bytes 196624 | tf_op jit(solution)/shard_map/reduce_scatter | solution.py:245
  674.1 45.8 %all-gather.35.cloned.1.call-done = bf16[2,2048,192]{1,2,0:T(8,128)(2,1)} async-done(((bf16[2,128,192]{1,2,0:T(8,128)(2,1)}), bf16[2,2048,192]{1,2,0:T(8,128)(2,1)}) %all-gather.35.cloned.1.call-update) | async-done | bytes 1572880 | tf_op jit(solution)/shard_map/all_gather | solution.py:222
  724.9 65.2 %while.55 = (s32[]{:T(128)}, f32[2,128,3,3,64]{1,4,3,2,0:T(8,128)}, f32[2,2048,3,64]{1,3,2,0:T(8,128)}, f32[2,2048,3,64]{1,3,2,0:T(8,128)}, bf16[2,2048,3,64]{1,...) while((s32[]{:T(128)}, f32[2,128,3,3,64]{1,4,3,2,0:T(8,128)}, ...), condition=%wide.region_22.23_spmd, body=%wide.region_20.22_spmd.sunk | while | flops 1546066816 | bytes 160072944 | solution.py:226
  732.8 11.3 fusion.341
  748.2 5.9 fusion.343
  766.0 11.0 fusion.341
  826.1 10.8 reduce-scatter.43.cloned.1.call-done
  839.6 137.1 %reduce-scatter.23.cloned.1.call-done = f32[2,128,192]{1,2,0:T(8,128)} async-done(((f32[2,2048,192]{1,2,0:T(8,128)}), f32[2,128,192]{1,2,0:T(8,128)}) %reduce-scatter.23.cloned.1.call-update) | async-done | bytes 196624 | tf_op jit(solution)/shard_map/reduce_scatter | solution.py:239
  978.7 8.4 reduce-scatter.47.cloned.1.call-done
  989.7 137.1 %reduce-scatter.25.cloned.1.call-done = f32[2,128,192]{1,2,0:T(8,128)} async-done(((f32[2,2048,192]{1,2,0:T(8,128)}), f32[2,128,192]{1,2,0:T(8,128)}) %reduce-scatter.25.cloned.1.call-update) | async-done | bytes 196624 | tf_op jit(solution)/shard_map/reduce_scatter | solution.py:245
  1128.8 8.3 reduce-scatter.51.cloned.1.call-done
  1139.6 9.2 reduce-scatter.31.cloned.1.call-done
  1150.6 10.0 reduce-scatter.35.cloned.1.call-done
  1170.8 45.1 %all-reduce.8 = (f32[1,288]{1,0:T(1,128)S(1)}, f32[1,288]{1,0:T(1,128)S(1)}, f32[1,288]{1,0:T(1,128)S(1)}, f32[1,288]{1,0:T(1,128)S(1)}) all-reduce(f32[1,288]{1,0:T(1,128)S(1)} %stack.82, f32[1,288]{1,0:T(1,128)S(1)} %stack.81, f32[1,288]{1,0:T(1,128)S(1)} %stack.97, ...), channel_id=1, replica_groups=mesh['ctx'=16,'fsdp'=2] {'ctx'}, use_global_device_ids=true, to_apply=%region_31.32 | all-reduce | flops 1152 | bytes 9216 | tf_op jit(solution)/shard_map/psum | solution.py:375
  1218.1 562.8 %all-reduce.14.cloned.1.call-done = (f32[1,288,576]{2,1,0:T(8,128)}, f32[1,288,576]{2,1,0:T(8,128)}, f32[1,288,192]{2,1,0:T(8,128)}, f32[1,288,192]{2,1,0:T(8,12...) async-done(((f32[1,288,576]{2,1,0:T(8,128)}, ...) | async-done | bytes 14155792 | tf_op jit(solution)/shard_map/psum | solution.py:375
  (629 shorter events, 377.0 us)
Async XLA Ops:
  7.2 142.6 %all-gather.29.cloned.1.call-start = ((), (), s32[]{:S(2)}) async-start(), calls=%async_computation.18 | async-start | bytes 1671168 | tf_op jit(solution)/shard_map/all_gather | solution.py:138
  18.9 146.8 %all-gather.37.cloned.1.call-start = ((), (), s32[]{:S(2)}) async-start(), calls=%async_computation.40 | async-start | bytes 2654208 | tf_op jit(solution)/shard_map/all_gather | solution.py:321
  21.9 147.4 %all-gather.39.cloned.1.call-start = ((), (), s32[]{:S(2)}) async-start(), calls=%async_computation.41 | async-start | bytes 2654208 | tf_op jit(solution)/shard_map/all_gather | solution.py:322
  23.3 150.0 %all-gather.41.cloned.1.call-start = ((), (), s32[]{:S(2)}) async-start(), calls=%async_computation.42 | async-start | bytes 2654208 | tf_op jit(solution)/shard_map/all_gather | solution.py:323
  26.2 161.2 %all-gather.47.cloned.1.call-start = ((), (), s32[]{:S(2)}) async-start(), calls=%async_computation.45 | async-start | bytes 2654208 | tf_op jit(solution)/shard_map/all_gather | solution.py:323
  32.8 58.6 %collective-permute-start = (bf16[2,128,192]{1,2,0:T(8,128)(2,1)}, bf16[2,128,192]{1,2,0:T(8,128)(2,1)}, u32[]{:S(2)}, u32[]{:S(2)}) collective-permute-start(bf16[2,128,192]{1,2,0:T(8,128)(2,1)} %bitcast.81), channel_id=1, source_target_pairs={{0,2},{2,4},{4,6},{6,8},{8,10},{10,12},{12,14},{14,16},{16,18},{18... | collective-permute-start | bytes 294920 | tf_op jit(solution)/shard_map/ppermute | solution.py:27
  35.6 55.9 %collective-permute-start.1 = (bf16[2,128,192]{1,2,0:T(8,128)(2,1)}, bf16[2,128,192]{1,2,0:T(8,128)(2,1)}, u32[]{:S(2)}, u32[]{:S(2)}) collective-permute-start(bf16[2,128,192]{1,2,0:T(8,128)(2,1)} %bitcast.81), channel_id=1, source_target_pairs={{0,30},{2,0},{4,2},{6,4},{8,6},{10,8},{12,10},{14,12},{16,14},{18,... | collective-permute-start | bytes 294920 | tf_op jit(solution)/shard_map/ppermute | solution.py:30
  39.7 224.6 %all-gather.31.cloned.1.call-start = ((), (), s32[]{:S(2)}) async-start(), calls=%async_computation.19 | async-start | bytes 1671168 | tf_op jit(solution)/shard_map/all_gather | solution.py:138
  177.3 104.5 %all-gather.45.cloned.1.call-start = ((), (), s32[]{:S(2)}) async-start(), calls=%async_computation.44 | async-start | bytes 2654208 | tf_op jit(solution)/shard_map/all_gather | solution.py:322
  178.1 107.3 %all-gather.43.cloned.1.call-start = ((), (), s32[]{:S(2)}) async-start(), calls=%async_computation.43 | async-start | bytes 2654208 | tf_op jit(solution)/shard_map/all_gather | solution.py:321
  178.9 145.5 %all-gather.33.cloned.1.call-start = ((), (), s32[]{:S(2)}) async-start(), calls=%async_computation.20 | async-start | bytes 1671168 | tf_op jit(solution)/shard_map/all_gather | solution.py:222
  191.7 10.8 collective-permute-start.16
  197.9 326.2 %reduce-scatter.19.cloned.1.call-start = ((), (), s32[]{:S(2)}) async-start(), calls=%async_computation.21 | async-start | bytes 3342336 | tf_op jit(solution)/shard_map/reduce_scatter | solution.py:239
  393.0 268.6 %reduce-scatter.21.cloned.1.call-start = ((), (), s32[]{:S(2)}) async-start(), calls=%async_computation.22 | async-start | bytes 3342336 | tf_op jit(solution)/shard_map/reduce_scatter | solution.py:245
  393.7 326.2 %all-gather.35.cloned.1.call-start = ((), (), s32[]{:S(2)}) async-start(), calls=%async_computation.23 | async-start | bytes 1671168 | tf_op jit(solution)/shard_map/all_gather | solution.py:222
  394.3 407.7 %reduce-scatter.29.cloned.1.call-start = ((), (), s32[]{:S(2)}) async-start(), calls=%async_computation.27 | async-start | bytes 1105920 | tf_op jit(solution)/shard_map/reduce_scatter | solution.py:350
  395.9 410.0 %reduce-scatter.41.cloned.1.call-start = ((), (), s32[]{:S(2)}) async-start(), calls=%async_computation.33 | async-start | bytes 1105920 | tf_op jit(solution)/shard_map/reduce_scatter | solution.py:359
  397.4 410.4 %reduce-scatter.53.cloned.1.call-start = ((), (), s32[]{:S(2)}) async-start(), calls=%async_computation.39 | async-start | bytes 2654208 | tf_op jit(solution)/shard_map/reduce_scatter | solution.py:371
  399.3 411.0 %reduce-scatter.45.cloned.1.call-start = ((), (), s32[]{:S(2)}) async-start(), calls=%async_computation.35 | async-start | bytes 2654208 | tf_op jit(solution)/shard_map/reduce_scatter | solution.py:365
  402.4 410.4 %reduce-scatter.49.cloned.1.call-start = ((), (), s32[]{:S(2)}) async-start(), calls=%async_computation.37 | async-start | bytes 2654208 | tf_op jit(solution)/shard_map/reduce_scatter | solution.py:368
  404.5 411.0 %reduce-scatter.33.cloned.1.call-start = ((), (), s32[]{:S(2)}) async-start(), calls=%async_computation.29 | async-start | bytes 442368 | tf_op jit(solution)/shard_map/reduce_scatter | solution.py:353
  673.9 143.3 %reduce-scatter.37.cloned.1.call-start = ((), (), s32[]{:S(2)}) async-start(), calls=%async_computation.31 | async-start | bytes 442368 | tf_op jit(solution)/shard_map/reduce_scatter | solution.py:356
  792.1 26.7 %reduce-scatter.27.cloned.1.call-start = ((), (), s32[]{:S(2)}) async-start(), calls=%async_computation.26 | async-start | bytes 1105920 | tf_op jit(solution)/shard_map/reduce_scatter | solution.py:350
  794.7 29.5 %reduce-scatter.39.cloned.1.call-start = ((), (), s32[]{:S(2)}) async-start(), calls=%async_computation.32 | async-start | bytes 1105920 | tf_op jit(solution)/shard_map/reduce_scatter | solution.py:359
  796.1 40.8 %reduce-scatter.43.cloned.1.call-start = ((), (), s32[]{:S(2)}) async-start(), calls=%async_computation.34 | async-start | bytes 2654208 | tf_op jit(solution)/shard_map/reduce_scatter | solution.py:365
  798.1 178.5 %reduce-scatter.23.cloned.1.call-start = ((), (), s32[]{:S(2)}) async-start(), calls=%async_computation.24 | async-start | bytes 3342336 | tf_op jit(solution)/shard_map/reduce_scatter | solution.py:239
  798.8 188.3 %reduce-scatter.47.cloned.1.call-start = ((), (), s32[]{:S(2)}) async-start(), calls=%async_computation.36 | async-start | bytes 2654208 | tf_op jit(solution)/shard_map/reduce_scatter | solution.py:368
  801.2 325.6 %reduce-scatter.25.cloned.1.call-start = ((), (), s32[]{:S(2)}) async-start(), calls=%async_computation.25 | async-start | bytes 3342336 | tf_op jit(solution)/shard_map/reduce_scatter | solution.py:245
  801.9 335.2 %reduce-scatter.51.cloned.1.call-start = ((), (), s32[]{:S(2)}) async-start(), calls=%async_computation.38 | async-start | bytes 2654208 | tf_op jit(solution)/shard_map/reduce_scatter | solution.py:371
  805.8 343.1 %reduce-scatter.31.cloned.1.call-start = ((), (), s32[]{:S(2)}) async-start(), calls=%async_computation.28 | async-start | bytes 442368 | tf_op jit(solution)/shard_map/reduce_scatter | solution.py:353
  978.7 181.9 %reduce-scatter.35.cloned.1.call-start = ((), (), s32[]{:S(2)}) async-start(), calls=%async_computation.30 | async-start | bytes 442368 | tf_op jit(solution)/shard_map/reduce_scatter | solution.py:356
  1128.8 652.1 %all-reduce.14.cloned.1.call-start = ((), (), s32[]{:S(2)}) async-start(), calls=%async_computation.46 | async-start | bytes 29491200 | tf_op jit(solution)/shard_map/psum | solution.py:375
  (154 other events, 2378.0 us)
Sparse Core Ops, SparseCore 0:
  19.0 59.4 all-gather.28
  80.6 8.2 all-gather.36
  91.1 11.2 all-gather.38
  103.7 11.2 all-gather.40
  117.0 11.2 all-gather.46
  177.5 60.9 all-gather.30
  240.6 9.0 all-gather.44
  251.7 11.2 all-gather.42
  266.3 57.9 all-gather.32
  393.1 130.9 reduce-scatter.18
  529.6 131.8 reduce-scatter.20
  664.1 55.7 all-gather.34
  722.2 6.2 reduce-scatter.28
  730.7 9.1 reduce-scatter.40
  742.0 10.3 reduce-scatter.52
  755.1 10.5 reduce-scatter.44
  767.8 10.5 reduce-scatter.48
  781.1 9.0 reduce-scatter.32
  792.4 8.8 reduce-scatter.36
  803.4 9.1 reduce-scatter.26
  814.9 9.2 reduce-scatter.38
  826.5 10.4 reduce-scatter.42
  842.5 134.0 reduce-scatter.22
  978.8 8.3 reduce-scatter.46
  992.7 134.0 reduce-scatter.24
  1128.9 8.1 reduce-scatter.50
  1139.8 9.0 reduce-scatter.30
  1151.7 8.8 reduce-scatter.34
  1168.2 612.6 all-reduce.13
